TPU v7x, 32 devices: a whole 2x2x4 slice. The times are simulated.
32 devices in a mesh: rows: 8 (over y, x, core), feat: 4 (over z).
Axes of the slice: x: 2, y: 2, z: 4, core: 2. Of those that a mesh axis runs over, the one named last changes fastest.
Arguments:
- features: bfloat16 [8192, 2048], P('rows', 'feat'), may hold values from -6 to 6
- grad_out: bfloat16 [8192, 2048], P('rows', 'feat'), may hold values from -6 to 6
- eigvecs: float32 [2048, 2048], P('feat', 'rows'), may hold values from -1 to 1, as said below
- eigvals: float32 [2048], replicated, may hold values from 0.1 to 1, as said below
- whiten: bfloat16 [2048, 2048], P(None, 'feat'), may hold values from -0.125 to 0.125
Outputs:
- grad_in: bfloat16 [8192, 2048], P('rows', 'feat')
Inputs may be any that keep to these rules, and one draw needn't show every extreme that they name: `eigvecs`: the columns are orthonormal. `eigvals`: any two entries differ by at least 0.45 / 2048.
All inputs are finite; a program needn't handle non-finite values.
Results may differ from a plain program's by a relative error of at most 0.0074.
Values may be sent and summed in bfloat16 or wider, within the bound.
A program may use at most 128 MiB of HBM per device.

v0:
```python
import jax
import jax.numpy as jnp
from jax import lax
from jax.sharding import PartitionSpec as P


def divided(lam_row, lam_col, first_col):
    on_diag = (
        jnp.arange(lam_row.shape[0], dtype=jnp.int32)[:, None]
        == (first_col + jnp.arange(lam_col.shape[0], dtype=jnp.int32))[None, :]
    )
    root_row = lam_row ** (-0.5)
    root_col = lam_col ** (-0.5)
    gaps_lam = lam_row[:, None] - lam_col[None, :]
    safe_gap = jnp.where(on_diag, jnp.ones_like(gaps_lam), gaps_lam)
    off_diag = (root_row[:, None] - root_col[None, :]) / safe_gap
    diag_vals = -0.5 * lam_row[:, None] ** (-1.5) + jnp.zeros_like(gaps_lam)
    return jnp.where(on_diag, diag_vals, off_diag)


def local(features, grad_out, eigvecs, eigvals, whiten):
    highest = lax.Precision.HIGHEST
    tok_rows, own_cols = features.shape
    row_count = tok_rows * lax.axis_size("rows")
    contract_rows = (((0,), (0,)), ((), ()))
    contract_last = (((1,), (1,)), ((), ()))
    piece_x = lax.all_gather(features, "feat", axis=1, tiled=True)
    piece_g = lax.all_gather(grad_out, "feat", axis=1, tiled=True)
    left_part = lax.dot_general(
        features, piece_g, contract_rows, preferred_element_type=jnp.float32
    )
    right_part = lax.dot_general(
        grad_out, piece_x, contract_rows, preferred_element_type=jnp.float32
    )
    cross_one = left_part
    cross_two = right_part
    sum_x = jnp.sum(piece_x, axis=0, dtype=jnp.float32)
    sum_g = jnp.sum(piece_g, axis=0, dtype=jnp.float32)
    cross_one, cross_two, sum_x, sum_g = (cross_one, cross_two, sum_x, sum_g)
    cross_one, cross_two, sum_x, sum_g = lax.psum((cross_one, cross_two, sum_x, sum_g), "rows")
    both_cross = cross_one + cross_two
    col_mean = sum_x / row_count
    grad_mean = sum_g / row_count
    offset = lax.axis_index("feat") * own_cols
    mean_part = lax.dynamic_slice_in_dim(col_mean, offset, own_cols)
    grad_part = lax.dynamic_slice_in_dim(grad_mean, offset, own_cols)
    sym_gram = 0.5 * (
        both_cross
        - row_count
        * (mean_part[:, None] * grad_mean[None, :] + grad_part[:, None] * col_mean[None, :])
    )
    basis_cols = lax.all_gather(eigvecs, "feat", axis=0, tiled=True)
    basis_block = lax.all_gather(eigvecs, "rows", axis=1, tiled=True)
    narrow = basis_cols.shape[1]
    inner_prod = jnp.dot(sym_gram, basis_cols, precision=highest)
    partial_value = lax.dot_general(basis_block, inner_prod, contract_rows, precision=highest)
    rotated = lax.psum(partial_value, "feat")
    first_col = lax.axis_index("rows") * narrow
    lam_col = lax.dynamic_slice_in_dim(eigvals, first_col, narrow)
    scaled = divided(eigvals, lam_col, first_col) * rotated
    back_rot = jnp.dot(basis_block, scaled, precision=highest)
    sens_own = lax.psum_scatter(
        lax.dot_general(back_rot, basis_cols, contract_last, precision=highest),
        "rows",
        scatter_dimension=0,
        tiled=True,
    )
    scaled_own = (2.0 / row_count * sens_own).astype(jnp.bfloat16)
    sens_scaled = lax.all_gather(scaled_own, "rows", axis=0, tiled=True)
    piece_x = lax.all_gather(features, "feat", axis=1, tiled=True)
    piece_g = lax.all_gather(grad_out, "feat", axis=1, tiled=True)
    shifted = (piece_g.astype(jnp.float32) - grad_mean).astype(jnp.bfloat16)
    centered = (piece_x.astype(jnp.float32) - col_mean).astype(jnp.bfloat16)
    running = jnp.dot(shifted, whiten, preferred_element_type=jnp.float32)
    grad_in = running + lax.dot_general(
        centered, sens_scaled, contract_last, preferred_element_type=jnp.float32
    )
    return grad_in.astype(jnp.bfloat16)


def solution(mesh):
    in_specs = (P("rows", "feat"), P("rows", "feat"), P("feat", "rows"), P(), P(None, "feat"))
    out_specs = P("rows", "feat")
    return jax.shard_map(local, mesh=mesh, in_specs=in_specs, out_specs=out_specs, check_vma=False)
```

profile of v0, /device:TPU:0, one launch (start us, length us, event | category | flops | bytes accessed | tf_op | source)
XLA Modules:
  0.0 552.3 jit_solution(13871746332786428748)
XLA Ops:
  6.5 0.0 copy-start
  6.5 0.0 all-gather.6.cloned.1.call-start
  6.5 0.7 all-gather.6.cloned.1.call-update
  7.3 0.0 all-gather.8.cloned.1.call-start
  7.3 0.7 all-gather.8.cloned.1.call-update
  8.0 0.0 all-gather.10.cloned.1.call-start
  8.1 0.7 all-gather.10.cloned.1.call-update
  8.7 0.0 copy-start.3
  8.8 0.0 all-reduce.6.cloned.1.call-start
  8.8 83.6 %all-gather.6.cloned.1.call-done = bf16[1024,2048]{1,0:T(8,128)(2,1)} async-done(((bf16[1024,512]{1,0:T(8,128)(2,1)}), bf16[1024,2048]{1,0:T(8,128)(2,1)}) %all-gather.6.cloned.1.call-update) | async-done | bytes 4194320 | tf_op jit(solution)/shard_map/all_gather | solution.py:71
  92.4 6.8 %fusion.40 = f32[512,2048]{1,0:T(8,128)} fusion(bf16[1024,512]{1,0:T(8,128)(2,1)} %param.5, bf16[1024,2048]{1,0:T(8,128)(2,1)} %all-gather.6.cloned.1.call-done), kind=kOutput, calls=%fused_computation.51 | convolution fusion | flops 2147483648 | bytes 9437184 | tf_op jit(solution)/shard_map/dot_general | solution.py:29
  99.2 74.0 %all-gather.8.cloned.1.call-done = bf16[1024,2048]{1,0:T(8,128)(2,1)} async-done(((bf16[1024,512]{1,0:T(8,128)(2,1)}), bf16[1024,2048]{1,0:T(8,128)(2,1)}) %all-gather.8.cloned.1.call-update) | async-done | bytes 4194320 | tf_op jit(solution)/shard_map/all_gather | solution.py:70
  173.2 0.0 copy-done.3
  173.2 7.8 %convolution_add_fusion = f32[512,2048]{1,0:T(8,128)} fusion(f32[512,2048]{1,0:T(8,128)} %fusion.40, bf16[1024,512]{1,0:T(8,128)(2,1)S(1)} %copy-done.3, bf16[1024,2048]{1,0:T(8,128)(2,1)} %all-gather.8.cloned.1.call-done), kind=kOutput, calls=%fused_computation.17 | convolution fusion | flops 2148532224 | bytes 13631488 | tf_op jit(solution)/shard_map/dot_general | solution.py:32
  181.0 0.0 all-reduce.6.cloned.1.call-update
  181.1 0.0 all-gather.12.cloned.1.call-start
  181.1 0.5 all-gather.12.cloned.1.call-update
  181.7 0.0 all-reduce.4.cloned.1.call-start
  181.7 0.0 copy-start.1
  181.7 3.0 convert_reduce_fusion
  184.7 0.5 copy-done.1
  185.2 0.6 convert_reduce_fusion.1
  185.8 25.6 %all-reduce = (f32[2048]{0:T(1024)S(1)}, f32[2048]{0:T(1024)S(1)}) all-reduce(f32[2048]{0:T(1024)S(1)} %convert_reduce_fusion, f32[2048]{0:T(1024)S(1)} %convert_reduce_fusion.1), channel_id=1, replica_groups=mesh['rows'=8,'feat'=4] {'rows'}, use_global_device_ids=true, to_apply=%region_3.0 | all-reduce | flops 4096 | bytes 32768 | tf_op jit(solution)/shard_map/psum | solution.py:40
  211.4 0.1 dynamic_slice.10
  211.5 0.1 dynamic_slice.11
  211.6 7.4 %all-gather.10.cloned.1.call-done = f32[2048,256]{1,0:T(8,128)} async-done(((f32[512,256]{1,0:T(8,128)}), f32[2048,256]{1,0:T(8,128)}) %all-gather.10.cloned.1.call-update) | async-done | bytes 2097168 | tf_op jit(solution)/shard_map/all_gather | solution.py:52
  219.0 82.8 %all-reduce.6.cloned.1.call-done = f32[512,2048]{1,0:T(8,128)} async-done(((f32[512,2048]{1,0:T(8,128)}), f32[512,2048]{1,0:T(8,128)}) %all-reduce.6.cloned.1.call-update) | async-done | bytes 4194320 | tf_op jit(solution)/shard_map/psum | solution.py:40
  301.7 6.9 %fusion.6 = f32[512,256]{1,0:T(8,128)S(1)} fusion(f32[2048,256]{1,0:T(8,128)} %all-gather.10.cloned.1.call-done, f32[512,2048]{1,0:T(8,128)} %all-reduce.6.cloned.1.call-done, f32[2048]{0:T(1024)S(1)} %get-tuple-element.11, f32[512]{0:T(512)S(1)} %dynamic_slice.11, f32[2048]{0:T(1024)S(1)} %get-tuple-element.12, f32[512]{0:T(512)S(1)} %dynamic_slice.10), kind=kOutput, calls=%fused_computation.8 | convolution fusion | flops 3227516928 | bytes 6836224 | tf_op jit(solution)/shard_map/dot_general | solution.py:55
  308.6 0.0 copy-start.5
  308.6 32.3 %all-gather.12.cloned.1.call-done = f32[512,2048]{1,0:T(8,128)} async-done(((f32[512,256]{1,0:T(8,128)}), f32[512,2048]{1,0:T(8,128)}) %all-gather.12.cloned.1.call-update) | async-done | bytes 4194320 | tf_op jit(solution)/shard_map/all_gather | solution.py:53
  340.9 10.2 %convolution_bitcast_fusion = f32[2048,256]{1,0:T(8,128)} fusion(f32[512,256]{1,0:T(8,128)S(1)} %fusion.6, f32[512,2048]{1,0:T(8,128)} %all-gather.12.cloned.1.call-done), kind=kOutput, calls=%fused_computation.18 | convolution fusion | flops 3221225472 | bytes 6815744 | tf_op jit(solution)/shard_map/dot_general | solution.py:56
  351.1 0.0 all-reduce.4.cloned.1.call-update
  351.1 0.3 reduce-scatter.2.cloned.1.call-start
  351.4 0.0 copy-done.5
  351.4 0.1 broadcast_power_fusion.1
  351.5 85.9 %all-reduce.4.cloned.1.call-done = f32[2048,256]{1,0:T(8,128)} async-done(((f32[2048,256]{1,0:T(8,128)}), f32[2048,256]{1,0:T(8,128)}) %all-reduce.4.cloned.1.call-update) | async-done | bytes 2097168 | tf_op jit(solution)/shard_map/psum | solution.py:57
  437.4 0.0 copy-start.4
  437.4 10.8 %fusion.15 = f32[256,512]{1,0:T(8,128)S(1)} fusion(f32[512,2048]{1,0:T(8,128)} %all-gather.12.cloned.1.call-done, f32[2048,256]{1,0:T(8,128)} %all-reduce.4.cloned.1.call-done, f32[256]{0:T(256)S(1)} %get-tuple-element.8, f32[2048]{0:T(1024)S(1)} %copy-done.5, f32[256]{0:T(256)S(1)} %get-tuple-element.7, f32[2048]{0:T(1024)S(1)} %get-tuple-element.10, ...), kind=kOutput, calls=%fused_computation.20 | convolution fusion | flops 3224895488 | bytes 6843392 | tf_op jit(solution)/shard_map/dot_general | solution.py:61
  448.2 0.0 copy-done.4
  448.2 8.4 %fusion.41 = f32[512,2048]{1,0:T(8,128)} fusion(f32[256,512]{1,0:T(8,128)S(1)} %fusion.15, f32[2048,256]{1,0:T(8,128)S(1)} %copy-done.4), kind=kOutput, calls=%fused_computation.52 | convolution fusion | flops 3221225472 | bytes 6815744 | tf_op jit(solution)/shard_map/dot_general | solution.py:63
  456.6 0.0 reduce-scatter.2.cloned.1.call-update
  456.7 0.3 all-gather.14.cloned.1.call-start
  457.0 50.0 %reduce-scatter.2.cloned.1.call-done = f32[64,2048]{1,0:T(8,128)} async-done(((f32[512,2048]{1,0:T(8,128)}), f32[64,2048]{1,0:T(8,128)}) %reduce-scatter.2.cloned.1.call-update) | async-done | bytes 524304 | tf_op jit(solution)/shard_map/reduce_scatter | solution.py:62
  507.0 1.8 multiply_convert_fusion
  508.8 0.0 all-gather.14.cloned.1.call-update
  508.8 27.9 %all-gather.14.cloned.1.call-done = bf16[512,2048]{1,0:T(8,128)(2,1)} async-done(((bf16[64,2048]{1,0:T(8,128)(2,1)}), bf16[512,2048]{1,0:T(8,128)(2,1)}) %all-gather.14.cloned.1.call-update) | async-done | bytes 2097168 | tf_op jit(solution)/shard_map/all_gather | solution.py:69
  536.7 0.0 copy-start.2
  536.7 5.4 fusion.2
  542.1 0.0 copy-done
  542.1 0.0 copy-done.2
  542.1 3.3 add_convert_fusion
  (3 shorter events, 0.0 us)
Async XLA Ops:
  6.5 535.6 %copy-start = (bf16[2048,512]{1,0:T(8,128)(2,1)S(1)}, bf16[2048,512]{1,0:T(8,128)(2,1)}, u32[]{:S(2)}) copy-start(bf16[2048,512]{1,0:T(8,128)(2,1)} %param.9) | copy-start | bytes 6291460
  6.5 85.9 %all-gather.6.cloned.1.call-start = ((), (), s32[]{:S(2)}) async-start(), calls=%async_computation.1 | async-start | bytes 5242880 | tf_op jit(solution)/shard_map/all_gather | solution.py:71
  7.3 166.0 %all-gather.8.cloned.1.call-start = ((), (), s32[]{:S(2)}) async-start(), calls=%async_computation.2 | async-start | bytes 5242880 | tf_op jit(solution)/shard_map/all_gather | solution.py:70
  8.0 211.0 %all-gather.10.cloned.1.call-start = ((), (), s32[]{:S(2)}) async-start(), calls=%async_computation.3 | async-start | bytes 2621440 | tf_op jit(solution)/shard_map/all_gather | solution.py:52
  8.7 164.5 %copy-start.3 = (bf16[1024,512]{1,0:T(8,128)(2,1)S(1)}, bf16[1024,512]{1,0:T(8,128)(2,1)}, u32[]{:S(2)}) copy-start(bf16[1024,512]{1,0:T(8,128)(2,1)} %param.6) | copy-start | bytes 3145732
  8.8 293.0 %all-reduce.6.cloned.1.call-start = ((), (), s32[]{:S(2)}) async-start(), calls=%async_computation.8 | async-start | bytes 8388608 | tf_op jit(solution)/shard_map/psum | solution.py:40
  181.1 159.9 %all-gather.12.cloned.1.call-start = ((), (), s32[]{:S(2)}) async-start(), calls=%async_computation.4 | async-start | bytes 4718592 | tf_op jit(solution)/shard_map/all_gather | solution.py:53
  181.7 255.8 %all-reduce.4.cloned.1.call-start = ((), (), s32[]{:S(2)}) async-start(), calls=%async_computation.5 | async-start | bytes 4194304 | tf_op jit(solution)/shard_map/psum | solution.py:57
  181.7 3.5 copy-start.1
  308.6 42.8 %copy-start.5 = (f32[2048]{0:T(1024)S(1)}, f32[2048]{0:T(1024)}, u32[]{:S(2)}) copy-start(f32[2048]{0:T(1024)} %param.8) | copy-start | bytes 24580
  351.1 155.9 %reduce-scatter.2.cloned.1.call-start = ((), (), s32[]{:S(2)}) async-start(), calls=%async_computation.6 | async-start | bytes 4718592 | tf_op jit(solution)/shard_map/reduce_scatter | solution.py:62
  437.4 10.8 %copy-start.4 = (f32[2048,256]{1,0:T(8,128)S(1)}, f32[2048,256]{1,0:T(8,128)}, u32[]{:S(2)}) copy-start(f32[2048,256]{1,0:T(8,128)} %all-gather.10.cloned.1.call-done) | copy-start | bytes 6291460
  456.7 80.1 %all-gather.14.cloned.1.call-start = ((), (), s32[]{:S(2)}) async-start(), calls=%async_computation.7 | async-start | bytes 2359296 | tf_op jit(solution)/shard_map/all_gather | solution.py:69
  536.7 5.4 copy-start.2
Sparse Core Ops, SparseCore 0:
  8.9 83.4 all-gather.5
  94.0 79.2 all-gather.7
  174.8 44.1 all-gather.9
  222.1 79.5 all-reduce.5
  303.5 37.3 all-gather.11
  351.3 86.1 all-reduce.3
  456.8 50.1 reduce-scatter.1
  508.9 27.7 all-gather.13
where the time goes:
time: 552 us
  waiting for transfers between devices  447 us (81%)
  matrix products  59.6 us (11%)
  blocking collectives  25.6 us (5%)
  between operations  13.6 us (2%)
    psum x1, waiting for transfers between devices, local(): rotated = lax.psum(partial_value, 'feat')  85.9 us
    all_gather x1, waiting for transfers between devices, local(): piece_g = lax.all_gather(grad_out, 'feat', axis=1, tiled=True)  83.6 us
    psum x1, waiting for transfers between devices, local(): lax.psum((cross_one, cross_two, sum_x, sum_g), 'rows')  82.8 us
    all_gather x1, waiting for transfers between devices, local(): piece_x = lax.all_gather(features, 'feat', axis=1, tiled=True)  74 us
    reduce_scatter x1, waiting for transfers between devices, local(): lax.psum_scatter(lax.dot_general(back_rot, basis_cols, contract_last, pre...  50 us
    all_gather x1, waiting for transfers between devices, local(): basis_block = lax.all_gather(eigvecs, 'rows', axis=1, tiled=True)  32.3 us
    all_gather x1, waiting for transfers between devices, local(): sens_scaled = lax.all_gather(scaled_own, 'rows', axis=0, tiled=True)  27.9 us
    psum x1, blocking collectives, local(): lax.psum((cross_one, cross_two, sum_x, sum_g), 'rows')  25.6 us
  transfers between devices with their start and end apart: 8, of which 8 were waited for; matrix products, arithmetic and copies ran while one was open for 5% of the time, Pallas kernels for 0%

commit v1 on v0

--- a/solution.py
+++ b/solution.py
@@ -68,7 +68,12 @@
     scaled_own = (2.0 / row_count * sens_own).astype(jnp.bfloat16)
     sens_scaled = lax.all_gather(scaled_own, "rows", axis=0, tiled=True)
     piece_x = lax.all_gather(features, "feat", axis=1, tiled=True)
-    piece_g = lax.all_gather(grad_out, "feat", axis=1, tiled=True)
+    ring = [grad_out]
+    for hop in range(3):
+        ring.append(lax.ppermute(ring[-1], "feat", [(dev, (dev + 1) % 4) for dev in range(4)]))
+    piece_g = jnp.roll(
+        jnp.concatenate(ring[::-1], axis=1), (lax.axis_index("feat") + 1) * ring[0].shape[1], axis=1
+    )
     shifted = (piece_g.astype(jnp.float32) - grad_mean).astype(jnp.bfloat16)
     centered = (piece_x.astype(jnp.float32) - col_mean).astype(jnp.bfloat16)
     running = jnp.dot(shifted, whiten, preferred_element_type=jnp.float32)

time: 552 us -> 596 us (1.080)
  waiting for transfers between devices: 447 us -> 469 us
  local copies, waits for them, and re-layouts: 0.75 us -> 17 us
    ppermute x0 -> x3, waiting for transfers between devices: none -> 51.3 us  [local(): lax.ppermute(ring[-1], 'feat', [(dev, (dev + 1) % 4) for dev in range(4)])]
    all_gather x1, waiting for transfers between devices: 27.9 us -> 0.01 us  [local(): sens_scaled = lax.all_gather(scaled_own, 'rows', axis=0, tiled=True)]
    unnamed x12 -> x17, local copies, waits for them, and re-layouts: 0.51 us -> 15.7 us
  transfers between devices with their start and end apart: 8 -> 11, of which waited for: 8 -> 9; matrix products, arithmetic and copies ran while one was open for 5% -> 7% of each run, Pallas kernels for 0% -> 0%
where the time goes in v1:
time: 596 us
  waiting for transfers between devices  469 us (79%)
  matrix products  62.7 us (11%)
  blocking collectives  25.6 us (4%)
  local copies, waits for them, and re-layouts  17 us (3%)
  between operations  13.6 us (2%)
    psum x1, waiting for transfers between devices, local(): rotated = lax.psum(partial_value, 'feat')  85.9 us
    all_gather x1, waiting for transfers between devices, local(): piece_g = lax.all_gather(grad_out, 'feat', axis=1, tiled=True)  83.6 us
    psum x1, waiting for transfers between devices, local(): lax.psum((cross_one, cross_two, sum_x, sum_g), 'rows')  82.8 us
    all_gather x1, waiting for transfers between devices, local(): piece_x = lax.all_gather(features, 'feat', axis=1, tiled=True)  74 us
    ppermute x3, waiting for transfers between devices, local(): lax.ppermute(ring[-1], 'feat', [(dev, (dev + 1) % 4) for dev in range(4)])  51.3 us
    reduce_scatter x1, waiting for transfers between devices, local(): lax.psum_scatter(lax.dot_general(back_rot, basis_cols, contract_last, pre...  49.8 us
    all_gather x1, waiting for transfers between devices, local(): basis_block = lax.all_gather(eigvecs, 'rows', axis=1, tiled=True)  31.4 us
    psum x1, blocking collectives, local(): lax.psum((cross_one, cross_two, sum_x, sum_g), 'rows')  25.6 us
  transfers between devices with their start and end apart: 11, of which 9 were waited for; matrix products, arithmetic and copies ran while one was open for 7% of the time, Pallas kernels for 0%

profile of v1, /device:TPU:0, one launch (start us, length us, event | category | flops | bytes accessed | tf_op | source)
XLA Modules:
  0.0 595.7 jit_solution(17819731853876072754)
XLA Ops:
  6.5 0.0 copy-start
  6.5 0.0 all-gather.6.cloned.1.call-start
  6.5 0.7 all-gather.6.cloned.1.call-update
  7.3 0.0 all-gather.8.cloned.1.call-start
  7.3 0.7 all-gather.8.cloned.1.call-update
  8.0 0.0 all-gather.10.cloned.1.call-start
  8.1 0.7 all-gather.10.cloned.1.call-update
  8.7 0.0 copy-start.2
  8.8 0.0 all-reduce.6.cloned.1.call-start
  8.8 83.6 %all-gather.6.cloned.1.call-done = bf16[1024,2048]{1,0:T(8,128)(2,1)} async-done(((bf16[1024,512]{1,0:T(8,128)(2,1)}), bf16[1024,2048]{1,0:T(8,128)(2,1)}) %all-gather.6.cloned.1.call-update) | async-done | bytes 4194320 | tf_op jit(solution)/shard_map/all_gather | solution.py:28
  92.4 6.8 %fusion.38 = f32[512,2048]{1,0:T(8,128)} fusion(bf16[1024,512]{1,0:T(8,128)(2,1)} %param.5, bf16[1024,2048]{1,0:T(8,128)(2,1)} %all-gather.6.cloned.1.call-done), kind=kOutput, calls=%fused_computation.60 | convolution fusion | flops 2147483648 | bytes 9437184 | tf_op jit(solution)/shard_map/dot_general | solution.py:29
  99.2 74.0 %all-gather.8.cloned.1.call-done = bf16[1024,2048]{1,0:T(8,128)(2,1)} async-done(((bf16[1024,512]{1,0:T(8,128)(2,1)}), bf16[1024,2048]{1,0:T(8,128)(2,1)}) %all-gather.8.cloned.1.call-update) | async-done | bytes 4194320 | tf_op jit(solution)/shard_map/all_gather | solution.py:70
  173.2 0.0 copy-done.2
  173.2 7.8 %convolution_add_fusion = f32[512,2048]{1,0:T(8,128)} fusion(f32[512,2048]{1,0:T(8,128)} %fusion.38, bf16[1024,512]{1,0:T(8,128)(2,1)S(1)} %copy-done.2, bf16[1024,2048]{1,0:T(8,128)(2,1)} %all-gather.8.cloned.1.call-done), kind=kOutput, calls=%fused_computation.17 | convolution fusion | flops 2148532224 | bytes 13631488 | tf_op jit(solution)/shard_map/dot_general | solution.py:32
  181.0 0.0 all-reduce.6.cloned.1.call-update
  181.1 0.0 all-gather.12.cloned.1.call-start
  181.1 0.5 all-gather.12.cloned.1.call-update
  181.6 0.0 all-reduce.4.cloned.1.call-start
  181.7 0.0 copy-start.1
  181.7 3.0 convert_reduce_fusion.1
  184.7 0.5 copy-done.1
  185.2 0.6 convert_reduce_fusion
  185.8 25.6 %all-reduce = (f32[2048]{0:T(1024)S(1)}, f32[2048]{0:T(1024)S(1)}) all-reduce(f32[2048]{0:T(1024)S(1)} %convert_reduce_fusion, f32[2048]{0:T(1024)S(1)} %convert_reduce_fusion.1), channel_id=1, replica_groups=mesh['rows'=8,'feat'=4] {'rows'}, use_global_device_ids=true, to_apply=%region_3.0 | all-reduce | flops 4096 | bytes 32768 | tf_op jit(solution)/shard_map/psum | solution.py:40
  211.4 0.1 dynamic_slice.15
  211.5 0.1 dynamic_slice.16
  211.6 7.4 %all-gather.10.cloned.1.call-done = f32[2048,256]{1,0:T(8,128)} async-done(((f32[512,256]{1,0:T(8,128)}), f32[2048,256]{1,0:T(8,128)}) %all-gather.10.cloned.1.call-update) | async-done | bytes 2097168 | tf_op jit(solution)/shard_map/all_gather | solution.py:52
  219.0 82.8 %all-reduce.6.cloned.1.call-done = f32[512,2048]{1,0:T(8,128)} async-done(((f32[512,2048]{1,0:T(8,128)}), f32[512,2048]{1,0:T(8,128)}) %all-reduce.6.cloned.1.call-update) | async-done | bytes 4194320 | tf_op jit(solution)/shard_map/psum | solution.py:40
  301.7 7.8 %fusion.4 = f32[512,256]{1,0:T(8,128)} fusion(f32[2048,256]{1,0:T(8,128)} %all-gather.10.cloned.1.call-done, f32[512,2048]{1,0:T(8,128)} %all-reduce.6.cloned.1.call-done, f32[2048]{0:T(1024)S(1)} %get-tuple-element.11, f32[512]{0:T(512)S(1)} %dynamic_slice.16, f32[2048]{0:T(1024)S(1)} %get-tuple-element.12, f32[512]{0:T(512)S(1)} %dynamic_slice.15), kind=kOutput, calls=%fused_computation.7 | convolution fusion | flops 3227516928 | bytes 6836224 | tf_op jit(solution)/shard_map/dot_general | solution.py:55
  309.6 0.0 copy-start.4
  309.6 31.4 %all-gather.12.cloned.1.call-done = f32[512,2048]{1,0:T(8,128)} async-done(((f32[512,256]{1,0:T(8,128)}), f32[512,2048]{1,0:T(8,128)}) %all-gather.12.cloned.1.call-update) | async-done | bytes 4194320 | tf_op jit(solution)/shard_map/all_gather | solution.py:53
  340.9 10.4 %convolution_bitcast_fusion = f32[2048,256]{1,0:T(8,128)} fusion(f32[512,256]{1,0:T(8,128)} %fusion.4, f32[512,2048]{1,0:T(8,128)} %all-gather.12.cloned.1.call-done), kind=kOutput, calls=%fused_computation.18 | convolution fusion | flops 3221225472 | bytes 6815744 | tf_op jit(solution)/shard_map/dot_general | solution.py:56
  351.3 0.0 all-reduce.4.cloned.1.call-update
  351.3 0.3 reduce-scatter.2.cloned.1.call-start
  351.6 0.0 copy-done.4
  351.6 0.1 broadcast_power_fusion.1
  351.7 85.9 %all-reduce.4.cloned.1.call-done = f32[2048,256]{1,0:T(8,128)} async-done(((f32[2048,256]{1,0:T(8,128)}), f32[2048,256]{1,0:T(8,128)}) %all-reduce.4.cloned.1.call-update) | async-done | bytes 2097168 | tf_op jit(solution)/shard_map/psum | solution.py:57
  437.6 0.0 copy-start.3
  437.6 10.8 %fusion.14 = f32[256,512]{1,0:T(8,128)S(1)} fusion(f32[512,2048]{1,0:T(8,128)} %all-gather.12.cloned.1.call-done, f32[2048,256]{1,0:T(8,128)} %all-reduce.4.cloned.1.call-done, f32[256]{0:T(256)S(1)} %get-tuple-element.8, f32[2048]{0:T(1024)S(1)} %copy-done.4, f32[256]{0:T(256)S(1)} %get-tuple-element.7, f32[2048]{0:T(1024)S(1)} %get-tuple-element.10, ...), kind=kOutput, calls=%fused_computation.20 | convolution fusion | flops 3224895488 | bytes 6843392 | tf_op jit(solution)/shard_map/dot_general | solution.py:61
  448.4 0.0 copy-done.3
  448.4 8.4 %fusion.39 = f32[512,2048]{1,0:T(8,128)} fusion(f32[256,512]{1,0:T(8,128)S(1)} %fusion.14, f32[2048,256]{1,0:T(8,128)S(1)} %copy-done.3), kind=kOutput, calls=%fused_computation.61 | convolution fusion | flops 3221225472 | bytes 6815744 | tf_op jit(solution)/shard_map/dot_general | solution.py:63
  456.8 0.0 reduce-scatter.2.cloned.1.call-update
  456.8 0.0 all-gather.14.cloned.1.call-start
  456.9 0.5 collective-permute-start
  457.3 49.8 %reduce-scatter.2.cloned.1.call-done = f32[64,2048]{1,0:T(8,128)} async-done(((f32[512,2048]{1,0:T(8,128)}), f32[64,2048]{1,0:T(8,128)}) %reduce-scatter.2.cloned.1.call-update) | async-done | bytes 524304 | tf_op jit(solution)/shard_map/reduce_scatter | solution.py:62
  507.2 1.8 multiply_convert_fusion
  508.9 0.0 all-gather.14.cloned.1.call-update
  509.0 0.0 collective-permute-done
  509.0 1.5 collective-permute-start.1
  510.5 25.4 %collective-permute-done.1 = bf16[1024,512]{1,0:T(8,128)(2,1)} collective-permute-done((bf16[1024,512]{1,0:T(8,128)(2,1)}, bf16[1024,512]{1,0:T(8,128)(2,1)}, u32[]{:S(2)}, u32[]{:S(2)}) %collective-permute-start.1) | collective-permute-done | bytes 1048608 | tf_op jit(solution)/shard_map/ppermute | solution.py:73
  535.9 0.0 collective-permute-start.2
  535.9 26.0 %collective-permute-done.2 = bf16[1024,512]{1,0:T(8,128)(2,1)} collective-permute-done((bf16[1024,512]{1,0:T(8,128)(2,1)}, bf16[1024,512]{1,0:T(8,128)(2,1)}, u32[]{:S(2)}, u32[]{:S(2)}) %collective-permute-start.2) | collective-permute-done | bytes 1048608 | tf_op jit(solution)/shard_map/ppermute | solution.py:73
  561.9 2.3 constant_dynamic-update-slice_fusion.7
  564.2 2.3 constant_dynamic-update-slice_fusion.6
  566.5 2.4 constant_dynamic-update-slice_fusion.5
  568.9 1.1 constant_dynamic-update-slice_fusion.4
  570.0 2.3 constant_dynamic-update-slice_fusion.3
  572.4 2.4 constant_dynamic-update-slice_fusion.2
  574.7 2.4 constant_dynamic-update-slice_fusion.1
  577.1 1.1 constant_dynamic-update-slice_fusion
  578.2 0.0 all-gather.14.cloned.1.call-done
  578.2 5.2 fusion.2
  583.4 0.0 copy-done
  583.4 5.5 add_convert_fusion
  (3 shorter events, 0.0 us)
Async XLA Ops:
  6.5 576.9 %copy-start = (bf16[2048,512]{1,0:T(8,128)(2,1)S(1)}, bf16[2048,512]{1,0:T(8,128)(2,1)}, u32[]{:S(2)}) copy-start(bf16[2048,512]{1,0:T(8,128)(2,1)} %param.9) | copy-start | bytes 6291460
  6.5 85.9 %all-gather.6.cloned.1.call-start = ((), (), s32[]{:S(2)}) async-start(), calls=%async_computation.1 | async-start | bytes 5242880 | tf_op jit(solution)/shard_map/all_gather | solution.py:28
  7.3 166.0 %all-gather.8.cloned.1.call-start = ((), (), s32[]{:S(2)}) async-start(), calls=%async_computation.2 | async-start | bytes 5242880 | tf_op jit(solution)/shard_map/all_gather | solution.py:70
  8.0 211.0 %all-gather.10.cloned.1.call-start = ((), (), s32[]{:S(2)}) async-start(), calls=%async_computation.3 | async-start | bytes 2621440 | tf_op jit(solution)/shard_map/all_gather | solution.py:52
  8.7 164.5 %copy-start.2 = (bf16[1024,512]{1,0:T(8,128)(2,1)S(1)}, bf16[1024,512]{1,0:T(8,128)(2,1)}, u32[]{:S(2)}) copy-start(bf16[1024,512]{1,0:T(8,128)(2,1)} %param.6) | copy-start | bytes 3145732
  8.8 293.0 %all-reduce.6.cloned.1.call-start = ((), (), s32[]{:S(2)}) async-start(), calls=%async_computation.8 | async-start | bytes 8388608 | tf_op jit(solution)/shard_map/psum | solution.py:40
  181.1 159.9 %all-gather.12.cloned.1.call-start = ((), (), s32[]{:S(2)}) async-start(), calls=%async_computation.4 | async-start | bytes 4718592 | tf_op jit(solution)/shard_map/all_gather | solution.py:53
  181.6 256.0 %all-reduce.4.cloned.1.call-start = ((), (), s32[]{:S(2)}) async-start(), calls=%async_computation.5 | async-start | bytes 4194304 | tf_op jit(solution)/shard_map/psum | solution.py:57
  181.7 3.5 copy-start.1
  309.6 42.0 %copy-start.4 = (f32[2048]{0:T(1024)S(1)}, f32[2048]{0:T(1024)}, u32[]{:S(2)}) copy-start(f32[2048]{0:T(1024)} %param.8) | copy-start | bytes 24580
  351.3 155.9 %reduce-scatter.2.cloned.1.call-start = ((), (), s32[]{:S(2)}) async-start(), calls=%async_computation.6 | async-start | bytes 4718592 | tf_op jit(solution)/shard_map/reduce_scatter | solution.py:62
  437.6 10.8 %copy-start.3 = (f32[2048,256]{1,0:T(8,128)S(1)}, f32[2048,256]{1,0:T(8,128)}, u32[]{:S(2)}) copy-start(f32[2048,256]{1,0:T(8,128)} %all-gather.10.cloned.1.call-done) | copy-start | bytes 6291460
  456.8 121.3 %all-gather.14.cloned.1.call-start = ((), (), s32[]{:S(2)}) async-start(), calls=%async_computation.7 | async-start | bytes 2359296 | tf_op jit(solution)/shard_map/all_gather | solution.py:69
  456.9 52.1 %collective-permute-start = (bf16[1024,512]{1,0:T(8,128)(2,1)S(1)}, bf16[1024,512]{1,0:T(8,128)(2,1)}, u32[]{:S(2)}, u32[]{:S(2)}) collective-permute-start(bf16[1024,512]{1,0:T(8,128)(2,1)S(1)} %copy-done.2), channel_id=1, source_target_pairs={{0,1},{1,2},{2,3},{3,0},{4,5},{5,6},{6,7},{7,4},{8,9},{9,10},{10,1... | collective-permute-start | bytes 3145736 | tf_op jit(solution)/shard_map/ppermute | solution.py:73
  509.0 26.9 %collective-permute-start.1 = (bf16[1024,512]{1,0:T(8,128)(2,1)}, bf16[1024,512]{1,0:T(8,128)(2,1)}, u32[]{:S(2)}, u32[]{:S(2)}) collective-permute-start(bf16[1024,512]{1,0:T(8,128)(2,1)} %collective-permute-done), channel_id=1, source_target_pairs={{0,1},{1,2},{2,3},{3,0},{4,5},{5,6},{6,7},{7,4},{8,9},{9,10},{10,1... | collective-permute-start | bytes 3145736 | tf_op jit(solution)/shard_map/ppermute | solution.py:73
  535.9 26.0 %collective-permute-start.2 = (bf16[1024,512]{1,0:T(8,128)(2,1)}, bf16[1024,512]{1,0:T(8,128)(2,1)}, u32[]{:S(2)}, u32[]{:S(2)}) collective-permute-start(bf16[1024,512]{1,0:T(8,128)(2,1)} %collective-permute-done.1), channel_id=1, source_target_pairs={{0,1},{1,2},{2,3},{3,0},{4,5},{5,6},{6,7},{7,4},{8,9},{9,10},{10,1... | collective-permute-start | bytes 3145736 | tf_op jit(solution)/shard_map/ppermute | solution.py:73
Sparse Core Ops, SparseCore 0:
  8.9 83.4 all-gather.5
  94.0 79.2 all-gather.7
  174.8 44.1 all-gather.9
  222.1 79.5 all-reduce.5
  303.5 37.3 all-gather.11
  351.4 86.1 all-reduce.3
  456.9 50.1 reduce-scatter.1
  509.1 27.7 all-gather.13
